TPU v7x, 32 devices: a whole 2x2x4 slice. The times are simulated.
32 devices in a mesh: replica: 8 (over z, y), model: 4 (over x, core).
Axes of the slice: x: 2, y: 2, z: 4, core: 2. Of those that a mesh axis runs over, the one named last changes fastest.
Arguments:
- partial_up: float32 [8, 1024, 4096], P('replica', None, 'model'), may hold values from -4 to 4
- partial_down: float32 [8, 4096, 1024], P('replica', 'model'), may hold values from -4 to 4
- partial_norm: float32 [8, 1024], P('replica'), may hold values from -8 to 8
- partial_bias: float32 [8, 1024], P('replica'), may hold values from -8 to 8
- master_up: float32 [1024, 4096], P('replica', 'model'), may hold values from -0.1875 to 0.1875
- master_down: float32 [4096, 1024], P('model', 'replica'), may hold values from -0.09375 to 0.09375
- master_norm: float32 [1024], P('replica'), may hold values from 0.25 to 1.75
- master_bias: float32 [1024], P('replica'), may hold values from -3 to 3
- memory_up: float32 [1024, 4096], P('replica', 'model'), may hold values from 0.05 to 0.8
- memory_down: float32 [4096, 1024], P('model', 'replica'), may hold values from 0.05 to 0.8
- memory_norm: float32 [1024], P('replica'), may hold values from 0.05 to 0.8
- memory_bias: float32 [1024], P('replica'), may hold values from 0.05 to 0.8
Outputs:
- compute_up: bfloat16 [1024, 4096], P(None, 'model')
- compute_down: bfloat16 [4096, 1024], P('model')
- compute_norm: bfloat16 [1024], replicated
- compute_bias: bfloat16 [1024], replicated
- stepped_up: float32 [1024, 4096], P('replica', 'model')
- stepped_down: float32 [4096, 1024], P('model', 'replica')
- stepped_norm: float32 [1024], P('replica')
- stepped_bias: float32 [1024], P('replica')
- state_new_up: float32 [1024, 4096], P('replica', 'model')
- state_new_down: float32 [4096, 1024], P('model', 'replica')
- state_new_norm: float32 [1024], P('replica')
- state_new_bias: float32 [1024], P('replica')
All inputs are finite; a program needn't handle non-finite values.
Results may differ from a plain program's by a relative error of at most 0.001.
Values may be sent and summed in bfloat16 or wider, within the bound.
A program may use at most 128 MiB of HBM per device.

v0:
```python
import functools
import math

import jax
import jax.numpy as jnp
from jax import lax
from jax.experimental import pallas as pl
from jax.experimental.pallas import tpu as pltpu
from jax.sharding import PartitionSpec as P

learn_rate = 0.05
hold_rate = 0.9


def plain(
    partial_up,
    partial_down,
    partial_norm,
    partial_bias,
    master_up,
    master_down,
    master_norm,
    master_bias,
    memory_up,
    memory_down,
    memory_norm,
    memory_bias,
):
    mean_up, mean_down = (
        lax.psum_scatter(partial_up[0], "replica", scatter_dimension=0, tiled=True),
        lax.psum_scatter(partial_down[0], "replica", scatter_dimension=1, tiled=True),
    )
    whole_norm, whole_bias = lax.psum((partial_norm[0], partial_bias[0]), "replica")
    place = lax.axis_index("replica")
    mean_norm = lax.dynamic_slice_in_dim(
        whole_norm, place * master_norm.shape[0], master_norm.shape[0]
    )
    mean_bias = lax.dynamic_slice_in_dim(
        whole_bias, place * master_bias.shape[0], master_bias.shape[0]
    )
    mean_rate = lax.axis_size("replica") ** (-0.5)
    mean_up = mean_up * mean_rate
    mean_down = mean_down * mean_rate
    mean_norm = mean_norm * mean_rate
    mean_bias = mean_bias * mean_rate
    state_new_up = hold_rate * memory_up + (1.0 - hold_rate) * mean_up * mean_up
    stepped_up = master_up - learn_rate * mean_up * lax.rsqrt(state_new_up + 1e-06)
    state_new_down = hold_rate * memory_down + (1.0 - hold_rate) * mean_down * mean_down
    stepped_down = master_down - learn_rate * mean_down * lax.rsqrt(state_new_down + 1e-06)
    state_new_norm = hold_rate * memory_norm + (1.0 - hold_rate) * mean_norm * mean_norm
    stepped_norm = master_norm - learn_rate * mean_norm * lax.rsqrt(state_new_norm + 1e-06)
    state_new_bias = hold_rate * memory_bias + (1.0 - hold_rate) * mean_bias * mean_bias
    stepped_bias = master_bias - learn_rate * mean_bias * lax.rsqrt(state_new_bias + 1e-06)
    compute_up, compute_down, compute_norm, compute_bias = (
        lax.all_gather(stepped_up.astype(jnp.bfloat16), "replica", axis=0, tiled=True),
        lax.all_gather(stepped_down.astype(jnp.bfloat16), "replica", axis=1, tiled=True),
        lax.all_gather(stepped_norm.astype(jnp.bfloat16), "replica", axis=0, tiled=True),
        lax.all_gather(stepped_bias.astype(jnp.bfloat16), "replica", axis=0, tiled=True),
    )
    return (
        compute_up,
        compute_down,
        compute_norm,
        compute_bias,
        stepped_up,
        stepped_down,
        stepped_norm,
        stepped_bias,
        state_new_up,
        state_new_down,
        state_new_norm,
        state_new_bias,
    )


SHARE = 3 / 4
SPAN = 124.0
POWER = 49
STEEP = 2.0 ** (2.0 * SPAN / POWER) - 1.0
LOW = 2.0 ** (-SPAN / POWER)
LAG_PAIR = 7
SUM_Y = (0, 4, 7, 10)
SUM_Z = (0, 4, 7, 11)
RELAY_Y = (0, 5, 8, 16)
RELAY_Z = (0, 21, 29, 48)
LAG_CLOSE = 4
LAG_SPREAD = 4
LAG_LAST = 2
LAG_VECTOR = 4
LAG_OWN = 4
LAG_NEAR = 9
HEAD_START = 2000
HOLD_Y = (1, 1, 0)
HOLD_Z = (14, 25, 0)
ORDER = ('rz', 'py', 'cy', 'a', 'cly', 'cz', 'spz', 'oz', 'clz', 'wy', 'oy', 'xz', 'f1', 'f', 'ry', 'ea')


def encode(x, reach):
    q = x * (LOW * STEEP / reach) + jnp.where(x < 0.0, -LOW, LOW)
    q2 = q * q
    q3 = q2 * q
    q6 = q3 * q3
    q12 = q6 * q6
    q24 = q12 * q12
    q48 = q24 * q24
    return (q48 * q).astype(jnp.bfloat16)


def decode(code, reach):
    y = code.astype(jnp.float32)
    grown = jnp.exp2(jnp.log(jnp.abs(y)) * (1.0 / (math.log(2.0) * POWER)))
    scale = reach / (LOW * STEEP)
    return (grown - LOW) * jnp.where(y < 0.0, -scale, scale)


def update(total, master, memory, rate):
    mean = total * rate
    state = hold_rate * memory + (1.0 - hold_rate) * mean * mean
    return master - learn_rate * mean * lax.rsqrt(state + 1e-06), state


def shares(hb):
    part_y = int(hb * SHARE) // 8 * 8
    cut_y, cut_z = -(-part_y // 32) * 16, (hb - part_y) // 32 * 16
    return (0, cut_y, part_y), (0, cut_z, hb - part_y)


def kernel(
    n,
    pu, pd, mu, md, su, sd, pn, pb, mn, mb, sn, sb,
    gy, gz, ou, od, qu, qd, cn, cb, step_s, state_s,
    xs, wu, wd, hu, hd,
    a_s, a_r, c_s0, c_s1, c_r0, c_r1, z_s0, z_s1, z_r0, z_r1, y_s, y_r,
    mine, theirs, packs, hold_s,
    sem_up, sem_down, sem_par, sem_vec,
    sa, ra, sc, rc, sz, rz, sy, ry, so, ro, st, rt, sf, rf, sg, rg, sp, rp, sq, rq, sv, rv, sw, rw,
):
    nz = n // 2
    tiles, _, hb, wide = xs.shape
    cuts_y, cuts_z = shares(hb)
    tiles_up = pu.shape[2] // wide
    me = lax.axis_index("replica")
    y = lax.rem(me, 2)
    row = lax.div(me, 2)
    other = me + 1 - 2 * y
    rate = n ** (-0.5)
    reach = n / 2.0
    c_s, c_r, z_s, z_r = (c_s0, c_s1), (c_r0, c_r1), (z_s0, z_s1), (z_r0, z_r1)

    def remote(src, dst, ss, rs, who):
        return pltpu.make_async_remote_copy(
            src_ref=src, dst_ref=dst, send_sem=ss, recv_sem=rs,
            device_id={"replica": who}, device_id_type=pl.DeviceIdType.MESH,
        )

    def load_up(k):
        lanes = pl.ds(pl.multiple_of(k * wide, wide), wide)
        return pltpu.make_async_copy(pu.at[:, :, lanes], xs.at[k], sem_up.at[k])

    def load_down(b):
        return pltpu.make_async_copy(
            pd.at[:, :, b * wide : (b + 1) * wide], xs.at[tiles_up:tiles, b], sem_down.at[b]
        )

    params = [
        pltpu.make_async_copy(a, b, sem_par.at[i])
        for i, (a, b) in enumerate(((mu, wu), (su, hu), (md, wd), (sd, hd)))
    ]
    vectors = [
        pltpu.make_async_copy(a, mine.at[at : at + a.shape[0], :], sem_vec.at[i])
        for i, (a, at) in enumerate(
            ((pn, 0), (pb, n), (mn, 2 * n), (mb, 2 * n + 1), (sn, 2 * n + 2), (sb, 2 * n + 3))
        )
    ]

    def rows_y(half):
        return slice(cuts_y[half], cuts_y[half + 1])

    def rows_z(half):
        return slice(cuts_z[half], cuts_z[half + 1])

    def rows_zx(half):
        return slice(cuts_y[2] + cuts_z[half], cuts_y[2] + cuts_z[half + 1])

    def encode_a(k, half):
        if half == 0:

            @pl.when(k < tiles_up)
            def _():
                load_up(k).wait()

            @pl.when(k == tiles_up)
            def _():
                for b in range(n):
                    load_down(b).wait()

        for t in range(nz):
            a_s[k, t, rows_y(half)] = encode(xs[k, 2 * t + 1 - y, rows_y(half), :], reach)

    load_up(0).start()
    barrier = pltpu.get_barrier_semaphore()
    pl.semaphore_signal(barrier, inc=1, device_id={"replica": other}, device_id_type=pl.DeviceIdType.MESH)

    @pl.when(row > 0)
    def _():
        pl.semaphore_signal(barrier, inc=1, device_id={"replica": me - 2}, device_id_type=pl.DeviceIdType.MESH)

    @pl.when(row < nz - 1)
    def _():
        pl.semaphore_signal(barrier, inc=1, device_id={"replica": me + 2}, device_id_type=pl.DeviceIdType.MESH)

    lax.fori_loop(1, tiles_up, lambda k, c: (load_up(k).start(), c)[1], 0)
    for p in params[:2]:
        p.start()
    mine[2 * n + 4 : 2 * n + 8, :] = jnp.zeros((4, wide), jnp.float32)
    for p in vectors:
        p.start()
    for b in range(n):
        load_down(b).start()
    for p in params[2:]:
        p.start()
    encode_a(jnp.int32(0), 0)

    def run(z):
        poses = (z, nz - 1 - z)
        far = max(poses)
        pl.semaphore_wait(barrier, 1 + (z > 0) + (z < nz - 1))
        pl.when(lax.rem(lax.axis_index("model"), 2) == 1)(lambda: pl.delay(HEAD_START))

        def beyond(d):
            return slice(z + 1, nz) if d == 0 else slice(0, z)

        def behind(d):
            return slice(0, z) if d == 0 else slice(z + 1, nz)

        def inward(d):
            return slice(z, nz) if d == 0 else slice(0, z + 1)

        def nextdev(d):
            return me + (2, -2)[d]

        def copy_a(k, half):
            r = rows_y(half)
            return remote(a_s.at[k, :, r], a_r.at[k, :, r], sa.at[0], ra.at[2 * k + half], other)

        def copy_c(k, half, d, sl):
            r = rows_y(half)
            return remote(c_s[d].at[k, sl, r], c_r[d].at[k, sl, r], sc.at[d], rc.at[d, 2 * k + half], nextdev(d))

        def copy_z(k, half, d, sl):
            r = rows_z(half)
            return remote(z_s[d].at[k, sl, :, r], z_r[d].at[k, sl, :, r], sz.at[d], rz.at[d, 2 * k + half], nextdev(d))

        def copy_y(k, half):
            r = rows_z(half)
            return remote(y_s.at[k, r], y_r.at[k, r], sy.at[0], ry.at[2 * k + half], other)

        def piece(ref, ss, rs, k, half, d):
            return remote(ref, ref, ss.at[d], rs.at[d, 2 * k + half], nextdev(d))

        def own_y(k, half, d, o):
            return piece(gy.at[k, o, y, rows_y(half)], so, ro, k, half, d)

        def rest_y(k, half, d, sl):
            return piece(gy.at[k, sl, y, rows_y(half)], st, rt, k, half, d)

        def fin_y(k, half, lo):
            ref = gy.at[k, lo : lo + 2, y, rows_y(half)]
            return remote(ref, ref, sf.at[0], rf.at[0], other)

        def side_z(k, half, who):
            ref = gz.at[k, z, who, rows_z(half)]
            return remote(ref, ref, sg.at[0], rg.at[2 * k + half], other)

        def own_z(k, half, d, o):
            return piece(gz.at[k, o, :, rows_z(half)], sp, rp, k, half, d)

        def rest_z(k, half, d, sl):
            return piece(gz.at[k, sl, :, rows_z(half)], sq, rq, k, half, d)

        def prior(d):
            return (z - 1, slice(0, z - 1)) if d == 0 else (z + 1, slice(z + 2, nz))

        def pair_y(k, half):
            r = rows_y(half)
            copy_a(k, half).wait_recv()
            for t in range(nz):
                at = (k, 2 * t + y, r)
                xs[at] = xs[at] + decode(a_r[k, t, r], reach)

        def chain_y(k, half, d):
            r = rows_y(half)
            pos = poses[d]
            if pos > 0:
                copy_c(k, half, d, inward(d)).wait_recv()
            for t in range(nz)[beyond(d)]:
                value = xs[k, 2 * t + y, r, :]
                if pos > 0:
                    value = value + decode(c_r[d][k, t, r], 2.0 * reach * pos)
                c_s[d][k, t, r] = encode(value, 2.0 * reach * (pos + 1))
            if pos < nz - 1:
                copy_c(k, half, d, beyond(d)).start()

        def finish(k, r, total, put, place):
            @pl.when(k < tiles_up)
            def _():
                spot = (r, pl.ds(pl.multiple_of(k * wide, wide), wide))
                stepped, state = update(total, wu[spot], hu[spot], rate)
                ou[spot] = stepped
                qu[spot] = state
                put[k, z, y, place] = stepped.astype(jnp.bfloat16)

            @pl.when(k >= tiles_up)
            def _():
                spot = pl.ds(pl.multiple_of((k - tiles_up) * hb + r.start, 8), r.stop - r.start)
                stepped, state = update(total, wd[spot, :], hd[spot, :], rate)
                od[spot, :] = stepped
                qd[spot, :] = state
                put[k, z, y, place] = stepped.astype(jnp.bfloat16)

        def close_y(k, half):
            r = rows_y(half)
            total = xs[k, me, r, :]
            for d in range(2):
                if poses[d] > 0:
                    total = total + decode(c_r[d][k, z, r], 2.0 * reach * poses[d])
            finish(k, r, total, gy, r)

        def send_y(k, half, d):
            own_y(k, half, d, z).start()

        def relay_y(k, half, d):
            pos = poses[d]
            sl = prior(d)[1]
            if pos > 1:
                rest_y(k, half, d, sl).wait_recv()
            if pos < nz - 1:
                rest_y(k, half, d, behind(d)).start()

        def heard_y(k, half, d):
            own_y(k, half, d, prior(d)[0]).wait_recv()

        def near_y(k, half):
            fin_y(k, half, z // 2 * 2).start()

        def last_y(k, half):
            for lo in range(0, nz, 2):
                if lo != z // 2 * 2:
                    fin_y(k, half, lo).start()

        def chain_z(k, half, d):
            r = rows_z(half)
            pos = poses[d]
            if pos > 0:
                copy_z(k, half, d, inward(d)).wait_recv()
            for t in range(nz)[beyond(d)]:
                for j in range(2):
                    value = xs[k, 2 * t + j, rows_zx(half), :]
                    if pos > 0:
                        value = value + decode(z_r[d][k, t, j, r], reach * pos)
                    z_s[d][k, t, j, r] = encode(value, reach * (pos + 1))
            if pos < nz - 1:
                copy_z(k, half, d, beyond(d)).start()

        def cross_z(k, half):
            r = rows_z(half)
            sums = []
            for who in (1 - y, y):
                total = xs[k, 2 * z + who, rows_zx(half), :]
                for d in range(2):
                    if poses[d] > 0:
                        total = total + decode(z_r[d][k, z, who, r], reach * poses[d])
                sums.append(total)
            y_s[k, r] = encode(sums[0], reach * nz)
            copy_y(k, half).start()
            xs[k, me, rows_zx(half), :] = sums[1]

        def close_z(k, half):
            r = rows_z(half)
            copy_y(k, half).wait_recv()
            total = xs[k, me, rows_zx(half), :] + decode(y_r[k, r], reach * nz)
            finish(k, rows_zx(half), total, gz, r)
            side_z(k, half, y).start()

        def spread_z(k, half):
            side_z(k, half, 1 - y).wait_recv()

        def send_z(k, half, d):
            own_z(k, half, d, z).start()

        def relay_z(k, half, d):
            pos = poses[d]
            o, sl = prior(d)
            own_z(k, half, d, o).wait_recv()
            if pos > 1:
                rest_z(k, half, d, sl).wait_recv()
            if pos < nz - 1:
                rest_z(k, half, d, behind(d)).start()

        def vec_send():
            for p in vectors:
                p.wait()
            remote(mine, theirs, sv.at[0], rv.at[0], other).start()

        def vec_pair():
            remote(mine, theirs, sv.at[0], rv.at[0], other).wait_recv()
            a, b = mine[...], theirs[...]
            packs[z, 0 : 2 * n, :] = a[0 : 2 * n, :] + b[0 : 2 * n, :]
            first = y == 0
            packs[z, 2 * n : 2 * n + 8, :] = jnp.concatenate(
                [
                    jnp.where(first, a[2 * n : 2 * n + 4, :], b[2 * n : 2 * n + 4, :]),
                    jnp.where(first, b[2 * n : 2 * n + 4, :], a[2 * n : 2 * n + 4, :]),
                ],
                axis=0,
            )

        def copy_v(d, sl):
            ref = packs.at[sl]
            return remote(ref, ref, sw.at[d], rw.at[d], nextdev(d))

        def through(d):
            return slice(0, z + 1) if d == 0 else slice(z, nz)

        def vec_chain(d):
            if poses[d] > 0:
                copy_v(d, behind(d)).wait_recv()
            if poses[d] < nz - 1:
                copy_v(d, through(d)).start()

        def vec_close():
            total = packs[0, 0 : 2 * n, :]
            for t in range(1, nz):
                total = total + packs[t, 0 : 2 * n, :]
            for t in range(nz):
                held = packs[t, 2 * n : 2 * n + 8, :]
                for j in range(2):
                    for i in range(4):
                        at = i * n + 2 * t + j
                        hold_s[at : at + 1, :] = held[4 * j + i : 4 * j + i + 1, :]
            stepped, state = update(total, hold_s[0 : 2 * n, :], hold_s[2 * n : 4 * n, :], rate)
            cn[...] = stepped[0:n].astype(jnp.bfloat16)
            cb[...] = stepped[n : 2 * n].astype(jnp.bfloat16)
            step_s[...] = stepped
            state_s[...] = state

        at_spread = LAG_PAIR + SUM_Y[nz - 1]
        at_close = LAG_PAIR + SUM_Y[far]
        side_sum = SUM_Z[far]
        side_close = side_sum + LAG_CLOSE
        side_open = side_close + LAG_SPREAD
        side_spread = SUM_Z[nz - 1] + LAG_CLOSE + LAG_SPREAD
        heard = {}
        for d in range(2):
            before = poses[d] - 1
            if before >= 0:
                heard[d] = LAG_PAIR + SUM_Y[max(before, nz - 1 - before)] + HOLD_Y[before] + LAG_OWN
        at_near = max(at_close, heard[1 - z % 2]) + LAG_NEAR
        tasks = {
            "wy": [(heard[d], functools.partial(heard_y, d=d)) for d in heard],
            "f1": [(at_near, near_y)],
            "a": [(0, lambda k, half: copy_a(k, half).start())],
            "ea": [(-1, encode_a)],
            "py": [(LAG_PAIR, pair_y)],
            "cy": [(LAG_PAIR + SUM_Y[poses[d]], functools.partial(chain_y, d=d)) for d in range(2)],
            "cly": [(at_close, close_y)],
            "oy": [(at_close + HOLD_Y[poses[d]], functools.partial(send_y, d=d)) for d in range(2) if poses[d] < nz - 1],
            "oz": [(side_open + HOLD_Z[poses[d]], functools.partial(send_z, d=d)) for d in range(2) if poses[d] < nz - 1],
            "ry": [(at_spread + RELAY_Y[poses[d]], functools.partial(relay_y, d=d)) for d in range(2) if poses[d] > 0],
            "f": [(at_spread + RELAY_Y[far] + LAG_LAST, last_y)],
            "cz": [(SUM_Z[poses[d]], functools.partial(chain_z, d=d)) for d in range(2)],
            "xz": [(side_sum, cross_z)],
            "clz": [(side_close, close_z)],
            "spz": [(side_open, spread_z)],
            "rz": [(side_spread + RELAY_Z[poses[d]], functools.partial(relay_z, d=d)) for d in range(2) if poses[d] > 0],
        }
        plan = [step for name in ORDER for step in tasks[name]]
        slots = 2 * tiles + max(lag for lag, _ in plan)
        vec_at = 2 + LAG_VECTOR
        extra = [(2, vec_send), (vec_at, vec_pair)]
        extra += [(vec_at + LAG_VECTOR * poses[d], functools.partial(vec_chain, d)) for d in range(2)]
        extra.append((vec_at + LAG_VECTOR * nz, vec_close))
        extra.append((min(at_close, side_close), lambda: [p.wait() for p in params] and None))

        def slot(v, carry):
            for i in range(2):
                for when, step in extra:
                    if when % 2 == i:
                        pl.when(v == when // 2)(step)

                for lag, task in plan:
                    half = (i - lag) % 2
                    k = v + (i - lag - half) // 2
                    pl.when(jnp.logical_and(k >= 0, k < tiles))(functools.partial(task, k, half))

            return carry

        lax.fori_loop(0, (slots + 1) // 2, slot, 0)

        remote(a_s, a_r, sa.at[0], ra.at[0], other).wait_send()
        for d in range(2):
            if poses[d] < nz - 1:
                remote(c_s[d].at[:, beyond(d)], c_r[d].at[:, beyond(d)], sc.at[d], rc.at[d, 0], other).wait_send()
                remote(z_s[d].at[:, beyond(d)], z_r[d].at[:, beyond(d)], sz.at[d], rz.at[d, 0], other).wait_send()
                ref = gy.at[:, z, y]
                remote(ref, ref, so.at[d], ro.at[d, 0], other).wait_send()
                ref = gz.at[:, z]
                remote(ref, ref, sp.at[d], rp.at[d, 0], other).wait_send()
                if poses[d] > 0:
                    ref = gy.at[:, behind(d), y]
                    remote(ref, ref, st.at[d], rt.at[d, 0], other).wait_send()
                    ref = gz.at[:, behind(d)]
                    remote(ref, ref, sq.at[d], rq.at[d, 0], other).wait_send()
                copy_v(d, through(d)).wait_send()
        remote(y_s, y_r, sy.at[0], ry.at[0], other).wait_send()
        ref = gz.at[:, z, y]
        remote(ref, ref, sg.at[0], rg.at[0], other).wait_send()
        remote(mine, theirs, sv.at[0], rv.at[0], other).wait_send()
        ref = gy.at[:, :, y]
        remote(ref, ref, sf.at[0], rf.at[0], other).wait_send()
        ref = gy.at[:, :, 1 - y]
        remote(ref, ref, sf.at[0], rf.at[0], other).wait_recv()

    for z in range(nz):
        pl.when(row == z)(functools.partial(run, z))


def leave(
    n, gy, gz, ou, od, qu, qd, cn, cb, step_s, state_s,
    cu, cd, tu, td, vu, vd, xcn, xcb, tn, tb, vn, vb, sem,
):
    me = lax.axis_index("replica")
    tiles, nz, _, part_y, wide = gy.shape
    tiles_up = cu.shape[3] // wide
    size = cu.shape[2]
    pairs = []
    for ref, lo, hi in ((gy, 0, part_y), (gz, part_y, size)):
        for k in range(tiles_up):
            pairs.append((ref.at[k], cu.at[:, :, lo:hi, k * wide : (k + 1) * wide]))
        for b in range(n):
            pairs.append((ref.at[tiles_up:tiles, b // 2, b % 2], cd.at[:, lo:hi, b * wide : (b + 1) * wide]))
    pairs += [(ou, tu), (od, td), (qu, vu), (qd, vd), (cn, xcn), (cb, xcb)]
    pairs += [(step_s.at[pl.ds(me, 1), :], tn), (step_s.at[pl.ds(me + n, 1), :], tb)]
    pairs += [(state_s.at[pl.ds(me, 1), :], vn), (state_s.at[pl.ds(me + n, 1), :], vb)]
    copies = [pltpu.make_async_copy(a, b, sem.at[i]) for i, (a, b) in enumerate(pairs)]
    for c in copies:
        c.start()
    for c in copies:
        c.wait()


def fused(
    n, partial_up, partial_down, partial_norm, partial_bias, master_up, master_down,
    master_norm, master_bias, memory_up, memory_down, memory_norm, memory_bias,
):
    nz = n // 2
    hb, w = master_up.shape
    rows, wide = master_down.shape
    cuts_y, cuts_z = shares(hb)
    part_y, part_z = cuts_y[2], cuts_z[2]
    tiles_up, tiles_down = w // wide, rows // hb
    tiles = tiles_up + tiles_down
    units = tiles * 2
    f32, b16 = jnp.float32, jnp.bfloat16
    line = lambda a: a.reshape(1, -1)
    operands = (
        partial_up[0].reshape(n, hb, w), partial_down[0].reshape(tiles_down, hb, n * wide),
        master_up, master_down, memory_up, memory_down,
        partial_norm.reshape(n, -1), partial_bias.reshape(n, -1),
        line(master_norm), line(master_bias), line(memory_norm), line(memory_bias),
    )
    S = jax.ShapeDtypeStruct
    shapes = (
        S((nz, 2, hb, w), b16), S((tiles_down, hb, n * wide), b16),
        S((hb, w), f32), S((rows, wide), f32), S((hb, w), f32), S((rows, wide), f32),
        S((n, wide), b16), S((n, wide), b16),
        S((1, wide), f32), S((1, wide), f32), S((1, wide), f32), S((1, wide), f32),
    )
    hbm = pl.BlockSpec(memory_space=pltpu.HBM)
    vm = pl.BlockSpec(memory_space=pltpu.VMEM)
    D = pltpu.SemaphoreType.DMA
    V = pltpu.VMEM
    one, two, each, both = D((1,)), D((2,)), D((units,)), D((2, units))
    held = pl.pallas_call(
        functools.partial(kernel, n),
        out_shape=(
            S((tiles, nz, 2, part_y, wide), b16), S((tiles, nz, 2, part_z, wide), b16),
            S((hb, w), f32), S((rows, wide), f32), S((hb, w), f32), S((rows, wide), f32),
            S((n, wide), b16), S((n, wide), b16), S((2 * n, wide), f32), S((2 * n, wide), f32),
        ),
        in_specs=[hbm] * 12,
        out_specs=[vm] * 10,
        scratch_shapes=[
            V((tiles, n, hb, wide), f32),
            V((hb, w), f32), V((rows, wide), f32), V((hb, w), f32), V((rows, wide), f32),
            *[V((tiles, nz, part_y, wide), b16)] * 6,
            *[V((tiles, nz, 2, part_z, wide), b16)] * 4,
            *[V((tiles, part_z, wide), b16)] * 2,
            V((2 * n + 8, wide), f32), V((2 * n + 8, wide), f32), V((nz, 2 * n + 8, wide), f32), V((4 * n, wide), f32),
            D((tiles_up,)), D((n,)), D((4,)), D((6,)),
            one, each, two, both, two, both, one, each, two, both, two, both,
            one, one, one, each, two, both, two, both, one, one, two, two,
        ],
        compiler_params=pltpu.CompilerParams(
            collective_id=0, has_side_effects=True, vmem_limit_bytes=28 * 1024 * 1024
        ),
    )(*[pltpu.with_memory_space_constraint(a, pltpu.HBM) for a in operands])
    cu, cd, tu, td, vu, vd, cn, cb, tn, tb, vn, vb = pl.pallas_call(
        functools.partial(leave, n),
        out_shape=shapes,
        in_specs=[vm] * 10,
        out_specs=[hbm] * 12,
        scratch_shapes=[D((2 * (tiles_up + n) + 10,))],
        compiler_params=pltpu.CompilerParams(vmem_limit_bytes=4 * 1024 * 1024),
    )(*held)
    flat = lambda a: a.reshape(-1)
    return (
        cu.reshape(n * hb, w), cd.reshape(rows, n * wide), flat(cn), flat(cb),
        tu, td, flat(tn), flat(tb), vu, vd, flat(vn), flat(vb),
    )


def on_device(*args):
    n = lax.axis_size("replica")
    (hb, w), (rows, wide) = args[4].shape, args[5].shape
    fits = n % 8 == 0 and n < 16 and wide == 128 and args[6].shape[0] == wide and args[7].shape[0] == wide
    fits = fits and hb % 64 == 0 and n // 2 == len(SUM_Y) and rows % hb == 0 and w % wide == 0
    return fused(n, *args) if fits else plain(*args)


def solution(mesh):
    in_specs = (
        P("replica", None, "model"),
        P("replica", "model", None),
        P("replica", None),
        P("replica", None),
        P("replica", "model"),
        P("model", "replica"),
        P("replica"),
        P("replica"),
        P("replica", "model"),
        P("model", "replica"),
        P("replica"),
        P("replica"),
    )
    out_specs = (
        P(None, "model"),
        P("model", None),
        P(),
        P(),
        P("replica", "model"),
        P("model", "replica"),
        P("replica"),
        P("replica"),
        P("replica", "model"),
        P("model", "replica"),
        P("replica"),
        P("replica"),
    )
    return jax.shard_map(
        on_device, mesh=mesh, in_specs=in_specs, out_specs=out_specs, check_vma=False
    )
```

profile of v0, /device:TPU:0, one launch (start us, length us, event | category | flops | bytes accessed | tf_op | source)
XLA Modules:
  0.0 88.4 jit_solution(3099463119924491424)
XLA Ops:
  0.6 84.7 %shard_map.211 = (bf16[16,4,2,96,128]{4,3,2,1,0:T(8,128)(2,1)S(1)}, bf16[16,4,2,32,128]{4,3,2,1,0:T(8,128)(2,1)S(1)}, f32[128,1024]{1,0:T(8,128)S(1)}, f32[1024,...) custom-call(f32[8,128,1024]{2,1,0:T(8,128)} %bitcast.16, ...), custom_call_target="tpu_custom_call" | custom-call | tf_op jit(solution)/shard_map/pallas_call | solution.py:584
  85.4 3.0 %shard_map.212 = (bf16[4,2,128,1024]{3,2,1,0:T(8,128)(2,1)}, bf16[8,128,1024]{2,1,0:T(8,128)(2,1)}, f32[128,1024]{1,0:T(8,128)}, f32[1024,128]{1,0:T(8,128)}, f3...) custom-call(bf16[16,4,2,96,128]{4,3,2,1,0:T(8,128)(2,1)S(1)} %get-tu, ...), custom_call_target="tpu_custom_call" | custom-call | tf_op jit(solution)/shard_map/pallas_call | solution.py:608
where the time goes:
time: 88.6 us; the launch traced here: 88.4 us
  Pallas kernels  87.8 us (99%)
    pallas_call x1, Pallas kernels, fused(): pl.pallas_call(functools.partial(kernel, n), out_shape=(S((tiles, nz, 2,...  84.7 us
    pallas_call x1, Pallas kernels, fused(): pl.pallas_call(functools.partial(leave, n), out_shape=shapes, in_specs=[v...  3.03 us

commit v1 on v0

--- a/solution.py
+++ b/solution.py
@@ -533,13 +533,13 @@
     tiles, nz, _, part_y, wide = gy.shape
     tiles_up = cu.shape[3] // wide
     size = cu.shape[2]
-    pairs = []
+    pairs = [(ou, tu), (od, td), (qu, vu), (qd, vd)]
     for ref, lo, hi in ((gy, 0, part_y), (gz, part_y, size)):
         for k in range(tiles_up):
             pairs.append((ref.at[k], cu.at[:, :, lo:hi, k * wide : (k + 1) * wide]))
         for b in range(n):
             pairs.append((ref.at[tiles_up:tiles, b // 2, b % 2], cd.at[:, lo:hi, b * wide : (b + 1) * wide]))
-    pairs += [(ou, tu), (od, td), (qu, vu), (qd, vd), (cn, xcn), (cb, xcb)]
+    pairs += [(cn, xcn), (cb, xcb)]
     pairs += [(step_s.at[pl.ds(me, 1), :], tn), (step_s.at[pl.ds(me + n, 1), :], tb)]
     pairs += [(state_s.at[pl.ds(me, 1), :], vn), (state_s.at[pl.ds(me + n, 1), :], vb)]
     copies = [pltpu.make_async_copy(a, b, sem.at[i]) for i, (a, b) in enumerate(pairs)]

time: 88.6 us -> 88.6 us (level)
  no operation moved by 1% of the time
where the time goes in v1:
time: 88.6 us; the launch traced here: 88.4 us
  Pallas kernels  87.7 us (99%)
    pallas_call x1, Pallas kernels, fused(): pl.pallas_call(functools.partial(kernel, n), out_shape=(S((tiles, nz, 2,...  84.7 us
    pallas_call x1, Pallas kernels, fused(): pl.pallas_call(functools.partial(leave, n), out_shape=shapes, in_specs=[v...  3.01 us

profile of v1, /device:TPU:0, one launch (start us, length us, event | category | flops | bytes accessed | tf_op | source)
XLA Modules:
  0.0 88.4 jit_solution(5731325912222292085)
XLA Ops:
  0.6 84.7 %shard_map.211 = (bf16[16,4,2,96,128]{4,3,2,1,0:T(8,128)(2,1)S(1)}, bf16[16,4,2,32,128]{4,3,2,1,0:T(8,128)(2,1)S(1)}, f32[128,1024]{1,0:T(8,128)S(1)}, f32[1024,...) custom-call(f32[8,128,1024]{2,1,0:T(8,128)} %bitcast.16, ...), custom_call_target="tpu_custom_call" | custom-call | tf_op jit(solution)/shard_map/pallas_call | solution.py:584
  85.4 3.0 %shard_map.212 = (bf16[4,2,128,1024]{3,2,1,0:T(8,128)(2,1)}, bf16[8,128,1024]{2,1,0:T(8,128)(2,1)}, f32[128,1024]{1,0:T(8,128)}, f32[1024,128]{1,0:T(8,128)}, f3...) custom-call(bf16[16,4,2,96,128]{4,3,2,1,0:T(8,128)(2,1)S(1)} %get-tu, ...), custom_call_target="tpu_custom_call" | custom-call | tf_op jit(solution)/shard_map/pallas_call | solution.py:608
